TPU v7x, 128 devices: a whole 4x4x4 slice. The times are simulated.
128 devices in a mesh: pod: 1, dp: 2 (over core), sp: 64 (over z, y, x).
Axes of the slice: x: 4, y: 4, z: 4, core: 2. Of those that a mesh axis runs over, the one named last changes fastest.
Arguments:
- x: bfloat16 [24, 128, 64, 1024], P(('pod', 'dp'), 'sp')
- norm_gain: bfloat16 [2, 2, 1024], replicated
- norm_shift: bfloat16 [2, 2, 1024], replicated
- w_qkv: bfloat16 [2, 3, 1024, 16, 64], replicated
- w_out: bfloat16 [2, 16, 64, 1024], replicated
- w_up: bfloat16 [2, 1024, 4096], replicated
- w_down: bfloat16 [2, 4096, 1024], replicated
Outputs:
- output: bfloat16 [24, 128, 64, 1024], P(('pod', 'dp'), 'sp')
All inputs are finite; a program needn't handle non-finite values.
Results may differ from a plain program's by a relative error of at most 0.0154772.
Values are sent between devices in bfloat16 or wider.
A program may use at most 1 GiB of HBM per device.

v0:
```python
import jax
import jax.numpy as jnp
from jax import lax
from jax.experimental import pallas as pl
from jax.experimental.pallas import tpu as pltpu
from jax.sharding import PartitionSpec as P

LN_EPS = 1e-6
F32 = jnp.float32
BF16 = jnp.bfloat16
D = 1024
FF = 4096
RANKS = 64
GROUPS = 3
ROWS = 8
TILE = 256
HALF = 512
SEND_STEP = 23
MESH = pl.DeviceIdType.MESH


def dot_nt(a, b):
    return lax.dot_general(a, b, (((1,), (1,)), ((), ())), preferred_element_type=F32)


def dot(a, b):
    return jnp.dot(a, b, preferred_element_type=F32)


def normalize(tok, gain, shift):
    mean = jnp.mean(tok, axis=-1, keepdims=True)
    cen = tok - mean
    var = jnp.mean(cen * cen, axis=-1, keepdims=True)
    return cen * lax.rsqrt(var + LN_EPS) * gain + shift


def kernel(x_hbm, ng_ref, ns_ref, wqkv_hbm, wo_hbm, wu_hbm, wd_hbm, y_hbm,
           wq0, wq1, wo, wu, wd, xb, yb, t_buf, i_buf, os_buf, or_buf,
           n_buf, qkv, o_buf, r_buf, g_buf, stage, gain, shift, bd_s, bd_t,
           wsem, xsem, ysem, lsem, ssem, rsem):
    me = lax.axis_index("sp")

    def weight_copies(j):
        return (
            pltpu.make_async_copy(wo_hbm.at[j], wo, wsem.at[2]),
            pltpu.make_async_copy(wu_hbm.at[j], wu, wsem.at[3]),
            pltpu.make_async_copy(wd_hbm.at[j], wd, wsem.at[4]),
        )

    def x_copy(i):
        return pltpu.make_async_copy(x_hbm.at[pl.ds(2 * i, 2)], xb.at[lax.rem(i, 2)], xsem.at[lax.rem(i, 2)])

    def y_copy(i):
        c, half = i // 2, lax.rem(i, 2)
        dst = y_hbm.at[pl.ds(4 * c, 4), :, pl.ds(pl.multiple_of(32 * half, 32), 32), :]
        return pltpu.make_async_copy(yb.at[half], dst, ysem.at[half])

    wq0_copy = pltpu.make_async_copy(wqkv_hbm.at[0], wq0, wsem.at[0])
    wq1_copy = pltpu.make_async_copy(wqkv_hbm.at[1], wq1, wsem.at[1])
    x_copy(0).start()
    wq0_copy.start()
    for copy in weight_copies(0):
        copy.start()
    wq1_copy.start()
    barrier = pltpu.get_barrier_semaphore()

    @pl.loop(1, RANKS)
    def _(i):
        pl.semaphore_signal(barrier, 1, device_id={"sp": lax.rem(me + i, RANKS)}, device_id_type=MESH)

    gain[...] = ng_ref[...].astype(F32)
    shift[...] = ns_ref[...].astype(F32)
    row = lax.broadcasted_iota(jnp.int32, (256, 256), 0)
    col = lax.broadcasted_iota(jnp.int32, (256, 256), 1)
    bd_s[...] = jnp.where(row // 64 == col // 64, 1.0, 0.0).astype(BF16)
    row = lax.broadcasted_iota(jnp.int32, (256, 128), 0)
    col = lax.broadcasted_iota(jnp.int32, (256, 128), 1)
    bd_t[...] = jnp.where(row // 128 == col // 64, 1.0, 0.0).astype(BF16)
    pl.semaphore_wait(barrier, RANKS - 1)

    def exchange(src, dst, c, k):
        pltpu.make_async_copy(src.at[c, me], dst.at[c, me], lsem.at[k, c]).start()

        @pl.loop(1, RANKS)
        def _(i):
            peer = lax.rem(me + lax.rem(i * SEND_STEP, RANKS), RANKS)
            pltpu.make_async_remote_copy(
                src_ref=src.at[c, peer], dst_ref=dst.at[c, me], send_sem=ssem.at[k, c], recv_sem=rsem.at[k, c],
                device_id={"sp": peer}, device_id_type=MESH).start()

    def arrived(dst, c, k):
        pltpu.make_async_copy(dst.at[c, 0], dst.at[c, 0], lsem.at[k, c]).wait()
        blocks = dst.at[c, pl.ds(0, RANKS - 1)]
        pltpu.make_async_copy(blocks, blocks, rsem.at[k, c]).wait()

    def stage_get(first, count, step):
        return jnp.concatenate([stage[b, pl.ds(first, count, stride=step), :] for b in range(8)], axis=1).astype(BF16)

    def stage_put(rows, first, value):
        for b in range(value.shape[1] // 128):
            stage[first + b, rows, :] = value[:, b * 128:b * 128 + 128]

    def regroup(dst, c):
        @pl.loop(0, RANKS, unroll=4)
        def _(p):
            dst[c, p] = stage_get(p, ROWS, RANKS)

    def spatial_attention():
        low = lax.broadcasted_iota(jnp.int32, (64, 128), 1) < 64

        @pl.loop(0, 4)
        def _(f):
            rows = pl.ds(pl.multiple_of(f * 64, 64), 64)
            bd = bd_s[...]
            for quad in range(4):
                c0 = quad * 256
                q = qkv[rows, c0:c0 + 256]
                k = qkv[rows, D + c0:D + c0 + 256]
                v = qkv[rows, 2 * D + c0:2 * D + c0 + 256]
                kb = jnp.concatenate([k, k, k, k], axis=0) * bd
                vb = jnp.concatenate([v, v, v, v], axis=0) * bd
                s = dot_nt(q, kb)
                parts = []
                for side in range(2):
                    sc = s[:, side * 128:side * 128 + 128]
                    m0 = jnp.max(jnp.where(low, sc, -jnp.inf), axis=-1, keepdims=True)
                    m1 = jnp.max(jnp.where(low, -jnp.inf, sc), axis=-1, keepdims=True)
                    e = jnp.exp((sc - jnp.where(low, m0, m1)) * 0.125)
                    d0 = jnp.sum(jnp.where(low, e, 0.0), axis=-1, keepdims=True)
                    d1 = jnp.sum(jnp.where(low, 0.0, e), axis=-1, keepdims=True)
                    parts.append((e * jnp.where(low, 1.0 / d0, 1.0 / d1)).astype(BF16))
                o_buf[rows, c0:c0 + 256] = dot(jnp.concatenate(parts, axis=1), vb).astype(BF16)

    def temporal_attention():
        @pl.loop(0, 4)
        def _(vid):
            rows = pl.ds(pl.multiple_of(vid * 128, 128), 128)
            bd = bd_t[...]
            for pair in range(8):
                c0 = pair * 128
                q = qkv[rows, c0:c0 + 128]
                k = qkv[rows, D + c0:D + c0 + 128]
                v = qkv[rows, 2 * D + c0:2 * D + c0 + 128]
                kb = jnp.concatenate([k, k], axis=0) * bd
                vb = jnp.concatenate([v, v], axis=0) * bd
                s = dot_nt(q, kb)
                parts = []
                for side in range(2):
                    sc = s[:, side * 128:side * 128 + 128]
                    e = jnp.exp((sc - jnp.max(sc, axis=-1, keepdims=True)) * 0.125)
                    parts.append((e * (1.0 / jnp.sum(e, axis=-1, keepdims=True))).astype(BF16))
                stage[pair, rows, :] = dot(jnp.concatenate(parts, axis=1), vb).astype(BF16).astype(F32)

    def spatial_front(i):
        slot = lax.rem(i, 2)
        x_copy(i).wait()

        @pl.when(i + 1 < 2 * GROUPS)
        def _():
            x_copy(i + 1).start()

        g1, s1 = gain[0, 0:1, :], shift[0, 0:1, :]

        @pl.loop(0, 4)
        def _(b):
            rows = pl.ds(pl.multiple_of(b * 64, 64), 64)
            tok = xb[slot, b // 2, lax.rem(b, 2)]
            r_buf[rows, :] = tok
            n_buf[rows, :] = normalize(tok.astype(F32), g1, s1).astype(BF16)

        @pl.when(i == 0)
        def _():
            wq0_copy.wait()

        @pl.loop(0, 6)
        def _(j):
            cols = pl.ds(pl.multiple_of(j * 512, 512), 512)
            qkv[0:TILE, cols] = dot_nt(n_buf[0:TILE, :], wq0[cols, :]).astype(BF16)

        spatial_attention()

    def tail_front(i):
        c, half = i // 2, lax.rem(i, 2)

        @pl.when(half == 0)
        def _():
            arrived(or_buf, c, 1)

        @pl.loop(0, 4)
        def _(b):
            rows = pl.ds(pl.multiple_of(b * 64, 64), 64)
            peers = pl.ds(half * 32 + b * 8, 8)
            r_buf[rows, :] = t_buf[c, peers].astype(F32).reshape(64, D).astype(BF16)
            o_buf[rows, :] = or_buf[c, peers].astype(F32).reshape(64, D).astype(BF16)

    def tail(j, base):
        for col in range(2):
            cols = slice(col * 512, col * 512 + 512)
            a = dot(o_buf[...], wo[:, cols]).astype(BF16)
            r_buf[:, cols] = (r_buf[:, cols].astype(F32) + a.astype(F32)).astype(BF16)
        g2, s2 = gain[j, 1:2, :], shift[j, 1:2, :]

        @pl.loop(0, 4)
        def _(b):
            rows = pl.ds(pl.multiple_of(b * 64, 64), 64)
            n_buf[rows, :] = normalize(r_buf[rows, :].astype(F32), g2, s2).astype(BF16)

        @pl.loop(0, 8)
        def _(k):
            cols = pl.ds(pl.multiple_of(k * 512, 512), 512)
            u = dot(n_buf[0:TILE, :], wu[:, cols]).astype(BF16)
            g_buf[:, cols] = jax.nn.gelu(u.astype(F32), approximate=True).astype(BF16)

        @pl.loop(0, 4)
        def _(k):
            cols = pl.ds(pl.multiple_of(k * 256, 256), 256)
            m = dot(g_buf[...], wd[:, cols]).astype(BF16)
            out = (r_buf[:, cols].astype(F32) + m.astype(F32)).astype(BF16)
            stage_put(pl.ds(base, TILE), 2 * k, out.astype(F32))

    def temporal(c):
        arrived(i_buf, c, 0)
        g1, s1 = gain[1, 0:1, :], shift[1, 0:1, :]

        @pl.loop(0, 8)
        def _(b):
            rows = pl.ds(pl.multiple_of(b * 64, 64), 64)
            tok = i_buf[c, pl.ds(b * 8, 8)].astype(F32).reshape(64, D)
            stage_put(rows, 0, normalize(tok, g1, s1))

        for r in range(ROWS):
            n_buf[r * 64:(r + 1) * 64, :] = stage_get(r, RANKS, ROWS)

        @pl.when(c == 0)
        def _():
            wq1_copy.wait()

        @pl.loop(0, 12)
        def _(j):
            cols = pl.ds(pl.multiple_of(j * 256, 256), 256)
            qkv[:, cols] = dot_nt(n_buf[...], wq1[cols, :]).astype(BF16)

        temporal_attention()
        regroup(os_buf, c)
        exchange(os_buf, or_buf, c, 1)

    def tail_back(i):
        half = lax.rem(i, 2)

        @pl.when(i >= 2)
        def _():
            y_copy(i - 2).wait()

        for r in range(ROWS):
            yb[half, r // 2, r % 2] = stage_get(r, 32, ROWS)
        y_copy(i).start()

    @pl.loop(0, 2 * GROUPS)
    def _(step):
        spatial = step < GROUPS

        @pl.loop(0, 2)
        def _(half):
            i = 2 * step + half

            @pl.when(spatial)
            def _():
                spatial_front(i)

            @pl.when(step >= GROUPS)
            def _():
                tail_front(i - 2 * GROUPS)

            @pl.when(jnp.logical_and(half == 0, jnp.logical_or(step == 0, step == GROUPS)))
            def _():
                for copy in weight_copies(0):
                    copy.wait()

            tail(jnp.where(spatial, 0, 1), pl.multiple_of(jnp.where(spatial, half * TILE, 0), TILE))

            @pl.when(step >= GROUPS)
            def _():
                tail_back(i - 2 * GROUPS)

        @pl.when(step == GROUPS - 1)
        def _():
            for copy in weight_copies(1):
                copy.start()

        @pl.when(spatial)
        def _():
            regroup(t_buf, step)
            exchange(t_buf, i_buf, step, 0)

        @pl.when(jnp.logical_and(step >= 1, step <= GROUPS))
        def _():
            temporal(step - 1)

    y_copy(2 * GROUPS - 2).wait()
    y_copy(2 * GROUPS - 1).wait()
    for k, buf in enumerate((t_buf, os_buf)):
        for c in range(GROUPS):
            blocks = buf.at[c, pl.ds(0, RANKS - 1)]
            pltpu.make_async_copy(blocks, blocks, ssem.at[k, c]).wait()


def solution(mesh):
    tok_spec = P(('pod', 'dp'), 'sp', None, None)
    hbm = pl.BlockSpec(memory_space=pl.ANY)
    vmem = pl.BlockSpec(memory_space=pltpu.VMEM)
    comm = pltpu.VMEM((GROUPS, RANKS, ROWS, D), BF16)

    call = pl.pallas_call(
        kernel,
        out_shape=jax.ShapeDtypeStruct((12, 2, 64, D), BF16),
        in_specs=[hbm, vmem, vmem, hbm, hbm, hbm, hbm],
        out_specs=hbm,
        scratch_shapes=[
            pltpu.VMEM((3 * D, D), BF16), pltpu.VMEM((3 * D, D), BF16),
            pltpu.VMEM((D, D), BF16), pltpu.VMEM((D, FF), BF16), pltpu.VMEM((FF, D), BF16),
            pltpu.VMEM((2, 2, 2, 64, D), BF16), pltpu.VMEM((2, 4, 2, 32, D), BF16),
            comm, comm, comm, comm,
            pltpu.VMEM((HALF, D), BF16), pltpu.VMEM((HALF, 3 * D), BF16), pltpu.VMEM((TILE, D), BF16),
            pltpu.VMEM((TILE, D), BF16), pltpu.VMEM((TILE, FF), BF16), pltpu.VMEM((8, HALF, 128), F32),
            pltpu.VMEM((2, 2, D), F32), pltpu.VMEM((2, 2, D), F32),
            pltpu.VMEM((256, 256), BF16), pltpu.VMEM((256, 128), BF16),
            pltpu.SemaphoreType.DMA((5,)), pltpu.SemaphoreType.DMA((2,)), pltpu.SemaphoreType.DMA((2,)),
            pltpu.SemaphoreType.DMA((2, GROUPS)), pltpu.SemaphoreType.DMA((2, GROUPS)),
            pltpu.SemaphoreType.DMA((2, GROUPS)),
        ],
        compiler_params=pltpu.CompilerParams(
            collective_id=0, has_side_effects=True, vmem_limit_bytes=66 * 1000 * 1000),
    )

    def local_step(x_loc, norm_gain, norm_shift, w_qkv, w_out, w_up, w_down):
        w_t = jnp.transpose(w_qkv, (0, 1, 3, 4, 2)).reshape(2, 3 * D, D)
        return call(x_loc, norm_gain, norm_shift, w_t, w_out.reshape(2, D, D), w_up, w_down)

    return jax.shard_map(local_step, mesh=mesh, in_specs=(tok_spec, P(), P(), P(), P(), P(), P()), out_specs=tok_spec, check_vma=False)
```

profile of v0, /device:TPU:1, one launch (start us, length us, event | category | flops | bytes accessed | tf_op | source)
XLA Modules:
  0.0 244.7 jit_solution(11023444805203025550)
XLA Ops:
  0.0 240.6 %shard_map.73 = bf16[12,2,64,1024]{3,2,1,0:T(8,128)(2,1)} custom-call(bf16[12,2,64,1024]{3,2,1,0:T(8,128)(2,1)} %x_hbm.1, bf16[2,2,1024]{2,1,0:T(2,128)(2,1)} %ng_ref.1, bf16[2,2,1024]{2,1,0:T(2,128)(2,1)} %ns_ref.1, bf16[2,3072,1024]{2,1,0:T(8,128)(2,1)} %bitcast.4, bf16[2,1024,1024]{2,1,0:T(8,128)(2,1)} %bitcast.5, bf16[2,1024,4096]{2,1,0:T(8,128)(2,1)} %wu_hbm.1, ...), custom_call_target="tpu_custom_call" | custom-call | tf_op jit(solution)/shard_map/pallas_call | solution.py:337
  240.6 4.0 %copy.9 = bf16[12,2,64,1024]{3,2,1,0:T(8,128)(2,1)} copy(bf16[12,2,64,1024]{3,2,1,0:T(8,128)(2,1)} %shard_map.73) | data formatting | bytes 6291456
where the time goes:
time: 245 us
  Pallas kernels  241 us (98%)
  local copies, waits for them, and re-layouts  4.03 us (2%)
    pallas_call x1, Pallas kernels, local_step(): call(x_loc, norm_gain, norm_shift, w_t, w_out.reshape(2, D, D), w_up, w_d...  241 us

commit v1 on v0

--- a/solution.py
+++ b/solution.py
@@ -16,6 +16,9 @@
 TILE = 256
 HALF = 512
 SEND_STEP = 23
+EXP_SCALE = 0.125 * 1.4426950408889634
+GELU_A = 0.7978845608028654
+GELU_B = GELU_A * 0.044715
 MESH = pl.DeviceIdType.MESH
 
 
@@ -25,6 +28,11 @@
 
 def dot(a, b):
     return jnp.dot(a, b, preferred_element_type=F32)
+
+
+def gelu(u):
+    half = 0.5 * u
+    return half + half * jnp.tanh(u * (GELU_A + GELU_B * (u * u)))
 
 
 def normalize(tok, gain, shift):
@@ -105,51 +113,72 @@
         def _(p):
             dst[c, p] = stage_get(p, ROWS, RANKS)
 
+    def pipelined(count, scores, probs, mix):
+        s, p = {}, {}
+        for t in range(count + 2):
+            if t < count:
+                s[t] = scores(t)
+            if 1 <= t <= count:
+                p[t - 1] = probs(s.pop(t - 1))
+            if t >= 2:
+                mix(t - 2, p.pop(t - 2))
+
     def spatial_attention():
         low = lax.broadcasted_iota(jnp.int32, (64, 128), 1) < 64
 
-        @pl.loop(0, 4)
-        def _(f):
-            rows = pl.ds(pl.multiple_of(f * 64, 64), 64)
-            bd = bd_s[...]
-            for quad in range(4):
-                c0 = quad * 256
-                q = qkv[rows, c0:c0 + 256]
-                k = qkv[rows, D + c0:D + c0 + 256]
-                v = qkv[rows, 2 * D + c0:2 * D + c0 + 256]
-                kb = jnp.concatenate([k, k, k, k], axis=0) * bd
-                vb = jnp.concatenate([v, v, v, v], axis=0) * bd
-                s = dot_nt(q, kb)
-                parts = []
-                for side in range(2):
-                    sc = s[:, side * 128:side * 128 + 128]
-                    m0 = jnp.max(jnp.where(low, sc, -jnp.inf), axis=-1, keepdims=True)
-                    m1 = jnp.max(jnp.where(low, -jnp.inf, sc), axis=-1, keepdims=True)
-                    e = jnp.exp((sc - jnp.where(low, m0, m1)) * 0.125)
-                    d0 = jnp.sum(jnp.where(low, e, 0.0), axis=-1, keepdims=True)
-                    d1 = jnp.sum(jnp.where(low, 0.0, e), axis=-1, keepdims=True)
-                    parts.append((e * jnp.where(low, 1.0 / d0, 1.0 / d1)).astype(BF16))
-                o_buf[rows, c0:c0 + 256] = dot(jnp.concatenate(parts, axis=1), vb).astype(BF16)
+        def spread(rows, c0):
+            t = qkv[rows, c0:c0 + 256]
+            return jnp.concatenate([t, t, t, t], axis=0) * bd_s[...]
+
+        def place(t):
+            return slice(t // 4 * 64, t // 4 * 64 + 64), t % 4 * 256
+
+        def scores(t):
+            rows, c0 = place(t)
+            return dot_nt(qkv[rows, c0:c0 + 256], spread(rows, D + c0))
+
+        def probs(s):
+            parts = []
+            for side in range(2):
+                sc = s[:, side * 128:side * 128 + 128]
+                m0 = jnp.max(jnp.where(low, sc, -jnp.inf), axis=-1, keepdims=True)
+                m1 = jnp.max(jnp.where(low, -jnp.inf, sc), axis=-1, keepdims=True)
+                e = jnp.exp2((sc - jnp.where(low, m0, m1)) * EXP_SCALE)
+                d0 = jnp.sum(jnp.where(low, e, 0.0), axis=-1, keepdims=True)
+                d1 = jnp.sum(jnp.where(low, 0.0, e), axis=-1, keepdims=True)
+                parts.append((e * jnp.where(low, 1.0 / d0, 1.0 / d1)).astype(BF16))
+            return jnp.concatenate(parts, axis=1)
+
+        def mix(t, p):
+            rows, c0 = place(t)
+            o_buf[rows, c0:c0 + 256] = dot(p, spread(rows, 2 * D + c0)).astype(BF16)
+
+        pipelined(16, scores, probs, mix)
 
     def temporal_attention():
         @pl.loop(0, 4)
         def _(vid):
             rows = pl.ds(pl.multiple_of(vid * 128, 128), 128)
-            bd = bd_t[...]
-            for pair in range(8):
-                c0 = pair * 128
-                q = qkv[rows, c0:c0 + 128]
-                k = qkv[rows, D + c0:D + c0 + 128]
-                v = qkv[rows, 2 * D + c0:2 * D + c0 + 128]
-                kb = jnp.concatenate([k, k], axis=0) * bd
-                vb = jnp.concatenate([v, v], axis=0) * bd
-                s = dot_nt(q, kb)
+
+            def spread(c0):
+                t = qkv[rows, c0:c0 + 128]
+                return jnp.concatenate([t, t], axis=0) * bd_t[...]
+
+            def scores(t):
+                return dot_nt(qkv[rows, t * 128:t * 128 + 128], spread(D + t * 128))
+
+            def probs(s):
                 parts = []
                 for side in range(2):
                     sc = s[:, side * 128:side * 128 + 128]
-                    e = jnp.exp((sc - jnp.max(sc, axis=-1, keepdims=True)) * 0.125)
+                    e = jnp.exp2((sc - jnp.max(sc, axis=-1, keepdims=True)) * EXP_SCALE)
                     parts.append((e * (1.0 / jnp.sum(e, axis=-1, keepdims=True))).astype(BF16))
-                stage[pair, rows, :] = dot(jnp.concatenate(parts, axis=1), vb).astype(BF16).astype(F32)
+                return jnp.concatenate(parts, axis=1)
+
+            def mix(t, p):
+                stage[t, rows, :] = dot(p, spread(2 * D + t * 128)).astype(BF16).astype(F32)
+
+            pipelined(8, scores, probs, mix)
 
     def spatial_front(i):
         slot = lax.rem(i, 2)
@@ -161,10 +190,9 @@
 
         g1, s1 = gain[0, 0:1, :], shift[0, 0:1, :]
 
-        @pl.loop(0, 4)
-        def _(b):
-            rows = pl.ds(pl.multiple_of(b * 64, 64), 64)
-            tok = xb[slot, b // 2, lax.rem(b, 2)]
+        for b in range(4):
+            rows = slice(b * 64, b * 64 + 64)
+            tok = xb[slot, b // 2, b % 2]
             r_buf[rows, :] = tok
             n_buf[rows, :] = normalize(tok.astype(F32), g1, s1).astype(BF16)
 
@@ -172,9 +200,8 @@
         def _():
             wq0_copy.wait()
 
-        @pl.loop(0, 6)
-        def _(j):
-            cols = pl.ds(pl.multiple_of(j * 512, 512), 512)
+        for j in range(6):
+            cols = slice(j * 512, j * 512 + 512)
             qkv[0:TILE, cols] = dot_nt(n_buf[0:TILE, :], wq0[cols, :]).astype(BF16)
 
         spatial_attention()
@@ -200,20 +227,20 @@
             r_buf[:, cols] = (r_buf[:, cols].astype(F32) + a.astype(F32)).astype(BF16)
         g2, s2 = gain[j, 1:2, :], shift[j, 1:2, :]
 
-        @pl.loop(0, 4)
-        def _(b):
-            rows = pl.ds(pl.multiple_of(b * 64, 64), 64)
+        for b in range(4):
+            rows = slice(b * 64, b * 64 + 64)
             n_buf[rows, :] = normalize(r_buf[rows, :].astype(F32), g2, s2).astype(BF16)
 
-        @pl.loop(0, 8)
-        def _(k):
-            cols = pl.ds(pl.multiple_of(k * 512, 512), 512)
-            u = dot(n_buf[0:TILE, :], wu[:, cols]).astype(BF16)
-            g_buf[:, cols] = jax.nn.gelu(u.astype(F32), approximate=True).astype(BF16)
-
-        @pl.loop(0, 4)
-        def _(k):
-            cols = pl.ds(pl.multiple_of(k * 256, 256), 256)
+        prev = None
+        for k in range(9):
+            cols = slice(k * 512, k * 512 + 512)
+            u = dot(n_buf[0:TILE, :], wu[:, cols]).astype(BF16) if k < 8 else None
+            if prev is not None:
+                g_buf[:, k * 512 - 512:k * 512] = gelu(prev.astype(F32)).astype(BF16)
+            prev = u
+
+        for k in range(4):
+            cols = slice(k * 256, k * 256 + 256)
             m = dot(g_buf[...], wd[:, cols]).astype(BF16)
             out = (r_buf[:, cols].astype(F32) + m.astype(F32)).astype(BF16)
             stage_put(pl.ds(base, TILE), 2 * k, out.astype(F32))
@@ -222,10 +249,10 @@
         arrived(i_buf, c, 0)
         g1, s1 = gain[1, 0:1, :], shift[1, 0:1, :]
 
-        @pl.loop(0, 8)
+        @pl.loop(0, 4)
         def _(b):
-            rows = pl.ds(pl.multiple_of(b * 64, 64), 64)
-            tok = i_buf[c, pl.ds(b * 8, 8)].astype(F32).reshape(64, D)
+            rows = pl.ds(pl.multiple_of(b * 128, 128), 128)
+            tok = i_buf[c, pl.ds(b * 16, 16)].astype(F32).reshape(128, D)
             stage_put(rows, 0, normalize(tok, g1, s1))
 
         for r in range(ROWS):
@@ -235,9 +262,8 @@
         def _():
             wq1_copy.wait()
 
-        @pl.loop(0, 12)
-        def _(j):
-            cols = pl.ds(pl.multiple_of(j * 256, 256), 256)
+        for j in range(12):
+            cols = slice(j * 256, j * 256 + 256)
             qkv[:, cols] = dot_nt(n_buf[...], wq1[cols, :]).astype(BF16)
 
         temporal_attention()

time: 245 us -> 166 us (0.68)
  Pallas kernels: 241 us -> 162 us
    pallas_call x1, Pallas kernels: 241 us -> 162 us  [local_step(): call(x_loc, norm_gain, norm_shift, w_t, w_out.reshape(2, D, D), w_up, w_d...]
where the time goes in v1:
time: 166 us
  Pallas kernels  162 us (98%)
  local copies, waits for them, and re-layouts  4.03 us (2%)
    pallas_call x1, Pallas kernels, local_step(): call(x_loc, norm_gain, norm_shift, w_t, w_out.reshape(2, D, D), w_up, w_d...  162 us
    unnamed x1, local copies, waits for them, and re-layouts  4.03 us

profile of v1, /device:TPU:1, one launch (start us, length us, event | category | flops | bytes accessed | tf_op | source)
XLA Modules:
  0.0 165.7 jit_solution(96076112561092087)
XLA Ops:
  0.0 161.6 %shard_map.73 = bf16[12,2,64,1024]{3,2,1,0:T(8,128)(2,1)} custom-call(bf16[12,2,64,1024]{3,2,1,0:T(8,128)(2,1)} %x_hbm.1, bf16[2,2,1024]{2,1,0:T(2,128)(2,1)} %ng_ref.1, bf16[2,2,1024]{2,1,0:T(2,128)(2,1)} %ns_ref.1, bf16[2,3072,1024]{2,1,0:T(8,128)(2,1)} %bitcast.4, bf16[2,1024,1024]{2,1,0:T(8,128)(2,1)} %bitcast.5, bf16[2,1024,4096]{2,1,0:T(8,128)(2,1)} %wu_hbm.1, ...), custom_call_target="tpu_custom_call" | custom-call | tf_op jit(solution)/shard_map/pallas_call | solution.py:363
  161.6 4.0 %copy.9 = bf16[12,2,64,1024]{3,2,1,0:T(8,128)(2,1)} copy(bf16[12,2,64,1024]{3,2,1,0:T(8,128)(2,1)} %shard_map.73) | data formatting | bytes 6291456
